TPU v7x, 32 devices: a whole 2x2x4 slice. The times are simulated.
32 devices in a mesh: seq: 8 (over z, y), head: 4 (over x, core).
Axes of the slice: x: 2, y: 2, z: 4, core: 2. Of those that a mesh axis runs over, the one named last changes fastest.
Arguments:
- image_patches: bfloat16 [8, 256, 1152], P('seq', None, 'head'), may hold values from -6 to 6
- text_embed: bfloat16 [2048, 2048], P('seq', 'head'), may hold values from -6 to 6
- image_start: int32 [8], replicated, may hold values from 0 to 30, as said below
- image_forget: float32 [8], replicated, may hold values from 0.001 to 0.3
- adapter: bfloat16 [1152, 2048], P('head'), may hold values from -0.1875 to 0.1875
- norm_gain: float32 [2048], replicated, may hold values from 0.5 to 1.5
- in_proj: bfloat16 [2048, 4, 2048], P(None, None, 'head'), may hold values from -0.125 to 0.125
- decay_proj: bfloat16 [2048, 16], P(None, 'head'), may hold values from -0.125 to 0.125
- head_decay_ceiling: float32 [16], P('head'), may hold values from 0 to 1, as said below
- out_gain: float32 [16, 128], P('head'), may hold values from 0.5 to 1.5
- out_proj: bfloat16 [2048, 2048], P('head'), may hold values from -0.125 to 0.125
Outputs:
- image_out: bfloat16 [8, 256, 2048], P('seq', None, 'head')
- text_out: bfloat16 [2048, 2048], P('seq', 'head')
Inputs may be any that keep to these rules, and one draw needn't show every extreme that they name: `image_start`: each entry is even; the images take distinct pairs of blocks. The merged piece of 512 tokens on one device of seq never holds both the image and the text that one device of seq holds in the source layout. `head_decay_ceiling`: Positive.
All inputs are finite; a program needn't handle non-finite values.
Results may differ from a plain program's by a relative error of at most 0.0095.
Values may be sent and summed in bfloat16 or wider, within the bound.
A program may use at most 128 MiB of HBM per device.

v0:
```python
import jax
import jax.numpy as jnp
from jax import lax
from jax.sharding import PartitionSpec as P

EPSILON = 1e-06


def prefix(array, axis, join, neutral):
    place = lax.axis_index(axis)
    gathered = jax.tree.map(
        lambda a, kind: lax.all_gather(a.astype(kind), axis), array, (jnp.bfloat16, jnp.bfloat16)
    )
    state = jax.tree.map(lambda a, e: jnp.zeros_like(a) + jnp.asarray(e, a.dtype), array, neutral)

    def one(step, state):
        return join(
            state,
            jax.tree.map(
                lambda a, own: lax.dynamic_index_in_dim(a, step, 0, False).astype(own.dtype),
                gathered,
                array,
            ),
        )

    return lax.fori_loop(0, place, one, state)


def rms_scale(values, gain_row):
    mean_square = jnp.mean(values * values, axis=-1, keepdims=True)
    return values * lax.rsqrt(mean_square + EPSILON) * gain_row


def shards(
    image_patches,
    text_embed,
    image_start,
    image_forget,
    adapter,
    norm_gain,
    in_proj,
    decay_proj,
    head_decay_ceiling,
    out_gain,
    out_proj,
):
    seq_count = lax.axis_size("seq")
    my_index = lax.axis_index("seq")
    patch_row_block = text_embed.shape[0]
    local_width = text_embed.shape[1]
    share_rows = patch_row_block // seq_count
    unit_count = 2 * seq_count
    token_rows = 2 * patch_row_block
    unit_ids = jnp.arange(unit_count, dtype=jnp.int32)
    device_ids = jnp.arange(seq_count, dtype=jnp.int32)
    unit_of_image = image_start // 2
    image_hits = (unit_of_image[:, None] == unit_ids[None, :]).astype(jnp.int32)
    is_image = jnp.sum(image_hits, axis=0)
    image_here = jnp.sum(image_hits * device_ids[:, None], axis=0)
    is_text = 1 - is_image
    text_here = jnp.cumsum(is_text) - is_text
    text_pick = ((is_text[None, :] == 1) & (text_here[None, :] == device_ids[:, None])).astype(
        jnp.int32
    )
    text_unit = jnp.sum(text_pick * unit_ids[None, :], axis=1)
    source = jnp.where(is_image == 1, image_here, text_here)
    my_units = 2 * my_index + jnp.arange(2, dtype=jnp.int32)
    unit_image = jnp.take(is_image, my_units)
    partial_value = jnp.dot(image_patches[0], adapter, preferred_element_type=jnp.float32)
    embedded = lax.psum_scatter(partial_value, "head", scatter_dimension=1, tiled=True).astype(
        jnp.bfloat16
    )
    units_here = jnp.stack([embedded, text_embed]).reshape(2, seq_count, share_rows, local_width)
    spread = lax.all_to_all(units_here, "seq", split_axis=1, concat_axis=1, tiled=True)
    table = spread.reshape(unit_count, share_rows, local_width)
    pick_index = is_text * seq_count + source
    outgoing_units = jnp.take(table, pick_index, axis=0).reshape(
        seq_count, 2, share_rows, local_width
    )
    arrived = lax.all_to_all(outgoing_units, "seq", split_axis=0, concat_axis=2, tiled=True)
    merged = arrived.reshape(token_rows, local_width)
    full_rows = lax.all_gather(merged, "head", axis=1, tiled=True)
    normed = rms_scale(full_rows.astype(jnp.float32), norm_gain).astype(jnp.bfloat16)
    model_width = in_proj.shape[0]
    head_count = head_decay_ceiling.shape[0]
    head_width = out_gain.shape[1]
    projected = jnp.dot(
        normed, in_proj.reshape(model_width, -1), preferred_element_type=jnp.float32
    )
    projected = projected.astype(jnp.bfloat16).reshape(token_rows, 4, head_count, head_width)
    gate_preactivation = jnp.dot(normed, decay_proj, preferred_element_type=jnp.float32)
    forget_element = jnp.where(
        unit_image == 1, jnp.log1p(-jnp.take(image_forget, jnp.take(image_here, my_units))), 0.0
    )
    start_offsets = jnp.arange(token_rows, dtype=jnp.int32) % patch_row_block == 0
    surge_logarithm = jnp.where(start_offsets, jnp.repeat(forget_element, patch_row_block), 0.0)
    decay_logarithm = (
        -head_decay_ceiling[None, :] * jax.nn.sigmoid(gate_preactivation) + surge_logarithm[:, None]
    )
    queries = projected[:, 0]
    key_rows = projected[:, 1]
    value_rows = projected[:, 2]
    gate_rows = projected[:, 3]
    within = jnp.cumsum(decay_logarithm, axis=0)
    span_decay = within[-1]
    scores = jnp.einsum("thd,shd->hts", queries, key_rows, preferred_element_type=jnp.float32)
    lagged = within.T[:, :, None] - within.T[:, None, :]
    row_ids = jnp.arange(token_rows, dtype=jnp.int32)
    causal = (row_ids[:, None] >= row_ids[None, :])[None]
    weights = jnp.where(causal, scores * jnp.exp(jnp.where(causal, lagged, 0.0)), 0.0).astype(
        jnp.bfloat16
    )
    inner_part = jnp.einsum("hts,shd->thd", weights, value_rows, preferred_element_type=jnp.float32)
    weighted_keys = key_rows.astype(jnp.float32) * jnp.exp(span_decay[None, :] - within)[:, :, None]
    local_state = jnp.einsum(
        "thd,the->hde",
        weighted_keys,
        value_rows.astype(jnp.float32),
        precision=lax.Precision.HIGHEST,
    )

    def combine(earlier, later_part):
        return (
            earlier[0] + later_part[0],
            jnp.exp(later_part[0])[:, None, None] * earlier[1] + later_part[1],
        )

    identity = (jnp.zeros_like(span_decay), jnp.zeros_like(local_state))
    decay_before, entering = prefix((span_decay, local_state), "seq", combine, identity)
    carried = jnp.exp(within)[:, :, None] * jnp.einsum(
        "thd,hde->the", queries.astype(jnp.float32), entering, precision=lax.Precision.HIGHEST
    )
    attended = inner_part + carried
    gated = rms_scale(attended, out_gain) * jax.nn.silu(gate_rows.astype(jnp.float32))
    gated = gated.astype(jnp.bfloat16).reshape(token_rows, -1)
    partial_out = jnp.dot(gated, out_proj, preferred_element_type=jnp.float32)
    summed = lax.psum_scatter(
        partial_out.astype(jnp.bfloat16), "head", scatter_dimension=1, tiled=True
    ).astype(jnp.float32)
    result = (merged.astype(jnp.float32) + summed).astype(jnp.bfloat16)
    result_shares = result.reshape(2, seq_count, share_rows, local_width)
    back_spread = lax.all_to_all(result_shares, "seq", split_axis=1, concat_axis=1, tiled=True)
    back_table = back_spread.reshape(unit_count, share_rows, local_width)
    wanted = jnp.stack([unit_of_image, text_unit], axis=1).reshape(-1)
    back_index = wanted % 2 * seq_count + wanted // 2
    outgoing = jnp.take(back_table, back_index, axis=0).reshape(
        seq_count, 2, share_rows, local_width
    )
    returned = lax.all_to_all(outgoing, "seq", split_axis=0, concat_axis=2, tiled=True)
    image_out = returned[:, 0]
    text_out = returned[0, 1]
    return (image_out, text_out)


def solution(mesh):
    in_specs = (
        P("seq", None, "head"),
        P("seq", "head"),
        P(),
        P(),
        P("head", None),
        P(),
        P(None, None, "head"),
        P(None, "head"),
        P("head"),
        P("head", None),
        P("head", None),
    )
    out_specs = (P("seq", None, "head"), P("seq", "head"))
    return jax.shard_map(shards, mesh=mesh, in_specs=in_specs, out_specs=out_specs, check_vma=False)
```

profile of v0, /device:TPU:0, one launch (start us, length us, event | category | flops | bytes accessed | tf_op | source)
XLA Modules:
  0.0 266.6 jit_solution(11392097754306038656)
XLA Ops:
  7.2 3.6 %fusion.25 = f32[256,2048]{1,0:T(8,128)} fusion(bf16[288,2048]{1,0:T(8,128)(2,1)} %param.21, bf16[1,256,288]{1,2,0:T(8,128)(2,1)} %param.17), kind=kOutput, calls=%fused_computation.50 | convolution fusion | flops 301989888 | bytes 3424256 | tf_op jit(solution)/shard_map/dot_general | solution.py:69
  10.8 34.0 %reduce-scatter.3.cloned.1.call-done = f32[256,512]{1,0:T(8,128)} async-done(((f32[256,2048]{1,0:T(8,128)}), f32[256,512]{1,0:T(8,128)}) %reduce-scatter.3.cloned.1.call-update) | async-done | bytes 524304 | tf_op jit(solution)/shard_map/reduce_scatter | solution.py:70
  44.9 1.1 convert_element_type.68
  46.0 0.8 pad_maximum_fusion
  46.8 5.6 %all-to-all-start = ((bf16[2,8,32,512]{3,2,0,1:T(8,128)(2,1)}), bf16[2,8,32,512]{3,2,0,1:T(8,128)(2,1)S(1)}, u32[]{:S(2)}, u32[]{:S(2)}) async-start(bf16[2,8,32,512]{3,2,0,1:T(8,128)(2,1)} %pad_maximum_fusion), calls=%async_computation.1 | async-start | bytes 1048576 | tf_op jit(solution)/shard_map/all_to_all | solution.py:74
  52.9 13.9 %all-to-all-done = bf16[2,8,32,512]{3,2,0,1:T(8,128)(2,1)S(1)} async-done(((bf16[2,8,32,512]{3,2,0,1:T(8,128)(2,1)}), bf16[2,8,32,512]{3,2,0,1:T(8,128)(2,1)S(1)}, u32[]{:S(2)}, u32[]{:S(2)}) %all-to-all-start) | async-done | bytes 524320 | tf_op jit(solution)/shard_map/all_to_all | solution.py:74
  67.6 18.0 %all_to_all.43 = bf16[8,2,32,512]{3,2,1,0:T(8,128)(2,1)S(1)} all-to-all(bf16[8,2,32,512]{3,2,1,0:T(8,128)(2,1)S(1)} %bitcast.109), channel_id=1, replica_groups=mesh['seq'=8,'head'=4] {'seq'}, dimensions={0} | all-to-all | bytes 1048576 | tf_op jit(solution)/shard_map/all_to_all | solution.py:80
  85.6 0.9 copy.135
  87.2 0.6 gather_fusion.2
  88.6 10.6 %copy.155 = bf16[256,8,4,512]{3,1,2,0:T(8,128)(2,1)} copy(bf16[256,8,4,512]{3,2,1,0:T(4,128)(2,1)} %bitcast.103) | data formatting | bytes 16777216
  99.2 8.1 %all-gather.5.cloned.1.call-done = bf16[512,2048]{1,0:T(8,128)(2,1)} async-done(((bf16[512,512]{1,0:T(8,128)(2,1)}), bf16[512,2048]{1,0:T(8,128)(2,1)}) %all-gather.5.cloned.1.call-update) | async-done | bytes 2097168 | tf_op jit(solution)/shard_map/all_gather | solution.py:82
  107.3 2.1 fusion
  109.4 2.3 fusion.12
  111.8 1.2 reduce-window.18
  113.7 9.9 %convolution_convert_fusion.1 = bf16[512,2048]{1,0:T(8,128)(2,1)} fusion(bf16[2048,2048]{1,0:T(8,128)(2,1)} %bitcast.104, bf16[512,2048]{1,0:T(8,128)(2,1)} %all-gather.5.cloned.1.call-done, f32[2048]{0:T(1024)S(1)} %copy-done.7, f32[512]{0:T(512)S(1)} %add_rsqrt_fusion.1), kind=kOutput, calls=%fused_computation.14 | convolution fusion | flops 4300210176 | bytes 12593152 | tf_op jit(solution)/shard_map/dot_general | solution.py:87
  123.5 4.4 %reshape.189 = bf16[512,4,4,128]{3,2,1,0:T(4,128)(2,1)} reshape(bf16[512,2048]{1,0:T(8,128)(2,1)} %convolution_convert_fusion.1) | data formatting | bytes 4194304 | tf_op jit(solution)/shard_map/reshape | solution.py:90
  128.0 3.2 %fusion.41 = (bf16[512,1,4,128]{3,2,1,0:T(4,128)(2,1)S(1)}, bf16[512,1,4,128]{3,2,1,0:T(4,128)(2,1)}, bf16[512,1,4,128]{3,2,1,0:T(4,128)(2,1)S(1)}, bf16[512,1,4,128]{3,2,1,0:T(4,128)(2,1)}) fusion(bf16[512,4,4,128]{3,2,1,0:T(4,128)(2,1)} %reshape.189), kind=kLoop, calls=%fused_computation.109 | loop fusion | bytes 4194304 | tf_op jit(solution)/shard_map/slice | solution.py:103
  131.2 1.1 copy.151
  132.3 3.2 %convolution_convert_fusion.2 = bf16[4,128,128]{2,1,0:T(8,128)(2,1)} fusion(bf16[512,1,4,128]{0,3,2,1:T(8,128)(2,1)} %copy.151, f32[512,4]{0,1:T(4,128)S(1)} %get-tuple-element.112, bf16[512,1,4,128]{3,2,1,0:T(4,128)(2,1)} %get-tuple-element.108), kind=kOutput, calls=%fused_computation.22 | convolution fusion | flops 403243008 | bytes 1187840 | tf_op jit(solution)/shard_map/thd,the->hde/dot_general | solution.py:115
  135.6 0.8 iota_compare_fusion
  136.5 20.7 %all-gather.1 = bf16[8,1,4]{2,1,0:T(2,128)(2,1)S(1)} all-gather(bf16[1,1,4]{2,1,0:T(2,128)(2,1)S(1)} %bitcast.124), channel_id=1, replica_groups=mesh['seq'=8,'head'=4] {'seq'}, dimensions={0}, use_global_device_ids=true | all-gather | bytes 72 | tf_op jit(solution)/shard_map/all_gather | solution.py:12
  157.7 4.4 %fusion.4 = f32[512,4,128]{0,2,1:T(8,128)} fusion(f32[4,512]{1,0:T(4,128)S(1)} %bitcast.120, pred[512,512]{1,0:T(8,128)(4,1)} %iota_compare_fusion, bf16[512,1,4,128]{0,3,2,1:T(8,128)(2,1)} %copy.151, bf16[512,1,4,128]{3,2,1,0:T(4,128)(2,1)} %get-tuple-element.106, bf16[512,1,4,128]{3,2,1,0:T(4,128)(2,1)} %get-tuple-element.108), kind=kOutput, calls=%fused_computation.16 | convolution fusion | flops 542113792 | bytes 2891776 | tf_op jit(solution)/shard_map/hts,shd->thd/dot_general | solution.py:113
  162.1 13.9 %all-gather.7.cloned.1.call-done = bf16[32,128,128]{2,1,0:T(8,128)(2,1)} async-done(((bf16[4,128,128]{2,1,0:T(8,128)(2,1)}), bf16[32,128,128]{2,1,0:T(8,128)(2,1)}) %all-gather.7.cloned.1.call-update) | async-done | bytes 1048592 | tf_op jit(solution)/shard_map/all_gather | solution.py:12
  176.1 2.0 multiply_reduce_fusion
  178.4 2.6 convolution_convert_fusion
  181.1 37.5 %reduce-scatter.5.cloned.1.call-done = bf16[512,512]{1,0:T(8,128)(2,1)} async-done(((bf16[512,2048]{1,0:T(8,128)(2,1)}), bf16[512,512]{1,0:T(8,128)(2,1)}) %reduce-scatter.5.cloned.1.call-update) | async-done | bytes 524304 | tf_op jit(solution)/shard_map/reduce_scatter | solution.py:137
  218.6 1.2 add_convert_fusion
  219.8 0.8 copy.145
  220.6 5.5 %all-to-all-start.2 = ((bf16[2,8,32,512]{3,2,0,1:T(8,128)(2,1)}), bf16[2,8,32,512]{3,2,0,1:T(8,128)(2,1)S(1)}, u32[]{:S(2)}, u32[]{:S(2)}) async-start(bf16[2,8,32,512]{3,2,0,1:T(8,128)(2,1)} %copy.145), calls=%async_computation.4 | async-start | bytes 1048576 | tf_op jit(solution)/shard_map/all_to_all | solution.py:142
  226.5 14.0 %all-to-all-done.2 = bf16[2,8,32,512]{3,2,0,1:T(8,128)(2,1)S(1)} async-done(((bf16[2,8,32,512]{3,2,0,1:T(8,128)(2,1)}), bf16[2,8,32,512]{3,2,0,1:T(8,128)(2,1)S(1)}, u32[]{:S(2)}, u32[]{:S(2)}) %all-to-all-start.2) | async-done | bytes 524320 | tf_op jit(solution)/shard_map/all_to_all | solution.py:142
  241.2 18.0 %all_to_all.44 = bf16[8,2,32,512]{3,2,1,0:T(8,128)(2,1)S(1)} all-to-all(bf16[8,2,32,512]{3,2,1,0:T(8,128)(2,1)S(1)} %bitcast.111), channel_id=1, replica_groups=mesh['seq'=8,'head'=4] {'seq'}, dimensions={0} | all-to-all | bytes 1048576 | tf_op jit(solution)/shard_map/all_to_all | solution.py:149
  259.3 0.8 slice_bitcast_fusion
  (78 shorter events, 5.7 us)
Async XLA Ops:
  7.2 171.3 %copy-start = (bf16[512,2048]{1,0:T(8,128)(2,1)S(1)}, bf16[512,2048]{1,0:T(8,128)(2,1)}, u32[]{:S(2)}) copy-start(bf16[512,2048]{1,0:T(8,128)(2,1)} %param.27) | copy-start | bytes 6291460
  7.2 38.8 %copy-start.4 = (bf16[256,512]{1,0:T(8,128)(2,1)S(1)}, bf16[256,512]{1,0:T(8,128)(2,1)}, u32[]{:S(2)}) copy-start(bf16[256,512]{1,0:T(8,128)(2,1)} %param.18) | copy-start | bytes 786436
  7.2 45.3 %copy-start.9 = (s32[8]{0:T(128)S(1)}, s32[8]{0:T(128)}, u32[]{:S(2)}) copy-start(s32[8]{0:T(128)} %param.19) | copy-start | bytes 100
  7.2 37.7 %reduce-scatter.3.cloned.1.call-start = ((), (), s32[]{:S(2)}) async-start(), calls=%async_computation.6 | async-start | bytes 2621440 | tf_op jit(solution)/shard_map/reduce_scatter | solution.py:70
  46.8 41.0 %copy-start.1 = (f32[8]{0:T(128)S(1)}, f32[8]{0:T(128)}, u32[]{:S(2)}) copy-start(f32[8]{0:T(128)} %param.20) | copy-start | bytes 100
  46.8 41.8 %copy-start.8 = (f32[4]{0:T(128)S(1)}, f32[4]{0:T(128)}, u32[]{:S(2)}) copy-start(f32[4]{0:T(128)} %param.25) | copy-start | bytes 52
  46.8 20.0 %all-to-all-start = ((bf16[2,8,32,512]{3,2,0,1:T(8,128)(2,1)}), bf16[2,8,32,512]{3,2,0,1:T(8,128)(2,1)S(1)}, u32[]{:S(2)}, u32[]{:S(2)}) async-start(bf16[2,8,32,512]{3,2,0,1:T(8,128)(2,1)} %pad_maximum_fusion), calls=%async_computation.1 | async-start | bytes 1048576 | tf_op jit(solution)/shard_map/all_to_all | solution.py:74
  52.5 54.8 %all-gather.5.cloned.1.call-start = ((), (), s32[]{:S(2)}) async-start(), calls=%async_computation.7 | async-start | bytes 2621440 | tf_op jit(solution)/shard_map/all_gather | solution.py:82
  86.5 89.5 %all-gather.7.cloned.1.call-start = ((), (), s32[]{:S(2)}) async-start(), calls=%async_computation.9 | async-start | bytes 1179648 | tf_op jit(solution)/shard_map/all_gather | solution.py:12
  88.6 20.8 %copy-start.6 = (bf16[2048,4]{0,1:T(4,128)(2,1)S(1)}, bf16[2048,4]{0,1:T(4,128)(2,1)}, u32[]{:S(2)}) copy-start(bf16[2048,4]{0,1:T(4,128)(2,1)} %param.24) | copy-start | bytes 49156
  88.6 20.8 %copy-start.7 = (f32[2048]{0:T(1024)S(1)}, f32[2048]{0:T(1024)}, u32[]{:S(2)}) copy-start(f32[2048]{0:T(1024)} %param.22) | copy-start | bytes 24580
  135.5 83.1 %reduce-scatter.5.cloned.1.call-start = ((), (), s32[]{:S(2)}) async-start(), calls=%async_computation.8 | async-start | bytes 2621440 | tf_op jit(solution)/shard_map/reduce_scatter | solution.py:137
  157.7 18.3 %copy-start.3 = (bf16[512,1,4,128]{3,2,1,0:T(4,128)(2,1)S(1)}, bf16[512,1,4,128]{3,2,1,0:T(4,128)(2,1)}, u32[]{:S(2)}) copy-start(bf16[512,1,4,128]{3,2,1,0:T(4,128)(2,1)} %get-tuple-element.106) | copy-start | bytes 1572868
  162.1 15.9 %copy-start.5 = (f32[4,128]{1,0:T(4,128)S(1)}, f32[4,128]{1,0:T(4,128)}, u32[]{:S(2)}) copy-start(f32[4,128]{1,0:T(4,128)} %param.26) | copy-start | bytes 6148
  178.4 40.2 %copy-start.2 = (bf16[1,2,8,32,512]{4,3,2,1,0:T(8,128)(2,1)S(1)}, bf16[1,2,8,32,512]{4,3,2,1,0:T(8,128)(2,1)}, u32[]{:S(2)}) copy-start(bf16[1,2,8,32,512]{4,3,2,1,0:T(8,128)(2,1)} %copy.135) | copy-start | bytes 1572868
  220.6 19.8 %all-to-all-start.2 = ((bf16[2,8,32,512]{3,2,0,1:T(8,128)(2,1)}), bf16[2,8,32,512]{3,2,0,1:T(8,128)(2,1)S(1)}, u32[]{:S(2)}, u32[]{:S(2)}) async-start(bf16[2,8,32,512]{3,2,0,1:T(8,128)(2,1)} %copy.145), calls=%async_computation.4 | async-start | bytes 1048576 | tf_op jit(solution)/shard_map/all_to_all | solution.py:142
Sparse Core Ops, SparseCore 0:
  11.0 33.8 reduce-scatter.2
  86.6 20.6 all-gather.4
  135.6 40.3 all-gather.6
  181.2 37.2 reduce-scatter.4
where the time goes:
time: 267 us
  waiting for transfers between devices  121 us (45%)
  blocking collectives  56.7 us (21%)
  matrix products  27.9 us (10%)
  local copies, waits for them, and re-layouts  26.5 us (10%)
  between operations  14.1 us (5%)
  starting transfers between devices  11.3 us (4%)
  other arithmetic  8.62 us (3%)
    reduce_scatter x1, waiting for transfers between devices, shards(): lax.psum_scatter(partial_out.astype(jnp.bfloat16), 'head', scatter_dimens...  37.5 us
    reduce_scatter x1, waiting for transfers between devices, shards(): lax.psum_scatter(partial_value, 'head', scatter_dimension=1, tiled=True)  34 us
    all_gather x1, blocking collectives, prefix(): lax.all_gather(a.astype(kind), axis)  20.7 us
    all_to_all x1, blocking collectives, shards(): lax.all_to_all(outgoing_units, 'seq', split_axis=0, concat_axis=2, tiled=...  18 us
    all_to_all x1, blocking collectives, shards(): lax.all_to_all(outgoing, 'seq', split_axis=0, concat_axis=2, tiled=True)  18 us
    all_to_all x1, waiting for transfers between devices, shards(): lax.all_to_all(result_shares, 'seq', split_axis=1, concat_axis=1, tiled=T...  14 us
    all_to_all x1, waiting for transfers between devices, shards(): lax.all_to_all(units_here, 'seq', split_axis=1, concat_axis=1, tiled=True)  13.9 us
    all_gather x1, waiting for transfers between devices, prefix(): lax.all_gather(a.astype(kind), axis)  13.9 us
  transfers between devices with their start and end apart: 6, of which 6 were waited for; matrix products, arithmetic and copies ran while one was open for 7% of the time, Pallas kernels for 0%

commit v1 on v0

--- a/solution.py
+++ b/solution.py
@@ -2,6 +2,7 @@
 import jax.numpy as jnp
 from jax import lax
 from jax.sharding import PartitionSpec as P
+from jax.lax import all_to_all, axis_size
 
 EPSILON = 1e-06
 
@@ -139,7 +140,10 @@
     ).astype(jnp.float32)
     result = (merged.astype(jnp.float32) + summed).astype(jnp.bfloat16)
     result_shares = result.reshape(2, seq_count, share_rows, local_width)
-    back_spread = lax.all_to_all(result_shares, "seq", split_axis=1, concat_axis=1, tiled=True)
+    side_arr = all_to_all(
+        jnp.stack(jnp.split(result_shares, axis_size("seq"), axis=1)), "seq", 0, 0
+    )
+    back_spread = jnp.concatenate(side_arr, axis=1)
     back_table = back_spread.reshape(unit_count, share_rows, local_width)
     wanted = jnp.stack([unit_of_image, text_unit], axis=1).reshape(-1)
     back_index = wanted % 2 * seq_count + wanted // 2

time: 267 us -> 272 us (1.019)
  local copies, waits for them, and re-layouts: 26.5 us -> 30.6 us
    unnamed x26 -> x33, local copies, waits for them, and re-layouts: 12.1 us -> 16.5 us
where the time goes in v1:
time: 272 us; the launch traced here: 271 us
  waiting for transfers between devices  121 us (44%)
  blocking collectives  56.7 us (21%)
  local copies, waits for them, and re-layouts  30.6 us (11%)
  matrix products  27.9 us (10%)
  between operations  14.1 us (5%)
  starting transfers between devices  11.3 us (4%)
  other arithmetic  8.63 us (3%)
    reduce_scatter x1, waiting for transfers between devices, shards(): lax.psum_scatter(partial_out.astype(jnp.bfloat16), 'head', scatter_dimens...  37.5 us
    reduce_scatter x1, waiting for transfers between devices, shards(): lax.psum_scatter(partial_value, 'head', scatter_dimension=1, tiled=True)  34 us
    all_gather x1, blocking collectives, prefix(): lax.all_gather(a.astype(kind), axis)  20.7 us
    all_to_all x1, blocking collectives, shards(): lax.all_to_all(outgoing_units, 'seq', split_axis=0, concat_axis=2, tiled=...  18 us
    all_to_all x1, blocking collectives, shards(): lax.all_to_all(outgoing, 'seq', split_axis=0, concat_axis=2, tiled=True)  18 us
    unnamed x33, local copies, waits for them, and re-layouts  16.5 us
    all_to_all x1, waiting for transfers between devices, shards(): all_to_all(jnp.stack(jnp.split(result_shares, axis_size('seq'), axis=1)),...  14 us
    all_to_all x1, waiting for transfers between devices, shards(): lax.all_to_all(units_here, 'seq', split_axis=1, concat_axis=1, tiled=True)  13.9 us
  transfers between devices with their start and end apart: 6, of which 6 were waited for; matrix products, arithmetic and copies ran while one was open for 7% of the time, Pallas kernels for 0%

profile of v1, /device:TPU:0, one launch (start us, length us, event | category | flops | bytes accessed | tf_op | source)
XLA Modules:
  0.0 270.8 jit_solution(12812521529179281891)
XLA Ops:
  7.2 3.6 %fusion.25 = f32[256,2048]{1,0:T(8,128)} fusion(bf16[288,2048]{1,0:T(8,128)(2,1)} %param.21, bf16[1,256,288]{1,2,0:T(8,128)(2,1)} %param.17), kind=kOutput, calls=%fused_computation.50 | convolution fusion | flops 301989888 | bytes 3424256 | tf_op jit(solution)/shard_map/dot_general | solution.py:70
  10.8 34.0 %reduce-scatter.3.cloned.1.call-done = f32[256,512]{1,0:T(8,128)} async-done(((f32[256,2048]{1,0:T(8,128)}), f32[256,512]{1,0:T(8,128)}) %reduce-scatter.3.cloned.1.call-update) | async-done | bytes 524304 | tf_op jit(solution)/shard_map/reduce_scatter | solution.py:71
  44.9 1.1 convert_element_type.68
  46.0 0.8 pad_maximum_fusion
  46.8 5.6 %all-to-all-start = ((bf16[2,8,32,512]{3,2,0,1:T(8,128)(2,1)}), bf16[2,8,32,512]{3,2,0,1:T(8,128)(2,1)S(1)}, u32[]{:S(2)}, u32[]{:S(2)}) async-start(bf16[2,8,32,512]{3,2,0,1:T(8,128)(2,1)} %pad_maximum_fusion), calls=%async_computation.1 | async-start | bytes 1048576 | tf_op jit(solution)/shard_map/all_to_all | solution.py:75
  52.9 13.9 %all-to-all-done = bf16[2,8,32,512]{3,2,0,1:T(8,128)(2,1)S(1)} async-done(((bf16[2,8,32,512]{3,2,0,1:T(8,128)(2,1)}), bf16[2,8,32,512]{3,2,0,1:T(8,128)(2,1)S(1)}, u32[]{:S(2)}, u32[]{:S(2)}) %all-to-all-start) | async-done | bytes 524320 | tf_op jit(solution)/shard_map/all_to_all | solution.py:75
  67.6 18.0 %all_to_all.43 = bf16[8,2,32,512]{3,2,1,0:T(8,128)(2,1)S(1)} all-to-all(bf16[8,2,32,512]{3,2,1,0:T(8,128)(2,1)S(1)} %bitcast.166), channel_id=1, replica_groups=mesh['seq'=8,'head'=4] {'seq'}, dimensions={0} | all-to-all | bytes 1048576 | tf_op jit(solution)/shard_map/all_to_all | solution.py:81
  85.6 0.9 copy.187
  86.6 0.6 gather_fusion.3
  87.2 0.6 gather_fusion.2
  88.6 10.6 %copy.222 = bf16[256,8,4,512]{3,1,2,0:T(8,128)(2,1)} copy(bf16[256,8,4,512]{3,2,1,0:T(4,128)(2,1)} %bitcast.153) | data formatting | bytes 16777216
  99.2 8.1 %all-gather.5.cloned.1.call-done = bf16[512,2048]{1,0:T(8,128)(2,1)} async-done(((bf16[512,512]{1,0:T(8,128)(2,1)}), bf16[512,2048]{1,0:T(8,128)(2,1)}) %all-gather.5.cloned.1.call-update) | async-done | bytes 2097168 | tf_op jit(solution)/shard_map/all_gather | solution.py:83
  107.3 2.1 fusion
  109.4 2.3 fusion.12
  111.8 1.2 reduce-window.18
  113.7 9.9 %convolution_convert_fusion.1 = bf16[512,2048]{1,0:T(8,128)(2,1)} fusion(bf16[2048,2048]{1,0:T(8,128)(2,1)} %bitcast.154, bf16[512,2048]{1,0:T(8,128)(2,1)} %all-gather.5.cloned.1.call-done, f32[2048]{0:T(1024)S(1)} %copy-done.7, f32[512]{0:T(512)S(1)} %add_rsqrt_fusion.1), kind=kOutput, calls=%fused_computation.14 | convolution fusion | flops 4300210176 | bytes 12593152 | tf_op jit(solution)/shard_map/dot_general | solution.py:88
  123.6 4.4 %reshape.189 = bf16[512,4,4,128]{3,2,1,0:T(4,128)(2,1)} reshape(bf16[512,2048]{1,0:T(8,128)(2,1)} %convolution_convert_fusion.1) | data formatting | bytes 4194304 | tf_op jit(solution)/shard_map/reshape | solution.py:91
  128.0 3.2 %fusion.49 = (bf16[512,1,4,128]{3,2,1,0:T(4,128)(2,1)S(1)}, bf16[512,1,4,128]{3,2,1,0:T(4,128)(2,1)}, bf16[512,1,4,128]{3,2,1,0:T(4,128)(2,1)S(1)}, bf16[512,1,4,128]{3,2,1,0:T(4,128)(2,1)}) fusion(bf16[512,4,4,128]{3,2,1,0:T(4,128)(2,1)} %reshape.189), kind=kLoop, calls=%fused_computation.125 | loop fusion | bytes 4194304 | tf_op jit(solution)/shard_map/slice | solution.py:104
  131.2 1.1 copy.210
  132.3 3.2 %convolution_convert_fusion.2 = bf16[4,128,128]{2,1,0:T(8,128)(2,1)} fusion(bf16[512,1,4,128]{0,3,2,1:T(8,128)(2,1)} %copy.210, f32[512,4]{0,1:T(4,128)S(1)} %get-tuple-element.112, bf16[512,1,4,128]{3,2,1,0:T(4,128)(2,1)} %get-tuple-element.108), kind=kOutput, calls=%fused_computation.22 | convolution fusion | flops 403243008 | bytes 1187840 | tf_op jit(solution)/shard_map/thd,the->hde/dot_general | solution.py:116
  135.6 0.8 iota_compare_fusion
  136.5 20.7 %all-gather.1 = bf16[8,1,4]{2,1,0:T(2,128)(2,1)S(1)} all-gather(bf16[1,1,4]{2,1,0:T(2,128)(2,1)S(1)} %bitcast.181), channel_id=1, replica_groups=mesh['seq'=8,'head'=4] {'seq'}, dimensions={0}, use_global_device_ids=true | all-gather | bytes 72 | tf_op jit(solution)/shard_map/all_gather | solution.py:13
  157.8 4.4 %fusion.4 = f32[512,4,128]{0,2,1:T(8,128)} fusion(f32[4,512]{1,0:T(4,128)S(1)} %bitcast.177, pred[512,512]{1,0:T(8,128)(4,1)} %iota_compare_fusion, bf16[512,1,4,128]{0,3,2,1:T(8,128)(2,1)} %copy.210, bf16[512,1,4,128]{3,2,1,0:T(4,128)(2,1)} %get-tuple-element.106, bf16[512,1,4,128]{3,2,1,0:T(4,128)(2,1)} %get-tuple-element.108), kind=kOutput, calls=%fused_computation.16 | convolution fusion | flops 542113792 | bytes 2891776 | tf_op jit(solution)/shard_map/hts,shd->thd/dot_general | solution.py:114
  162.2 13.8 %all-gather.7.cloned.1.call-done = bf16[32,128,128]{2,1,0:T(8,128)(2,1)} async-done(((bf16[4,128,128]{2,1,0:T(8,128)(2,1)}), bf16[32,128,128]{2,1,0:T(8,128)(2,1)}) %all-gather.7.cloned.1.call-update) | async-done | bytes 1048592 | tf_op jit(solution)/shard_map/all_gather | solution.py:13
  176.0 2.0 multiply_reduce_fusion
  178.4 2.6 convolution_convert_fusion
  181.1 37.5 %reduce-scatter.5.cloned.1.call-done = bf16[512,512]{1,0:T(8,128)(2,1)} async-done(((bf16[512,2048]{1,0:T(8,128)(2,1)}), bf16[512,512]{1,0:T(8,128)(2,1)}) %reduce-scatter.5.cloned.1.call-update) | async-done | bytes 524304 | tf_op jit(solution)/shard_map/reduce_scatter | solution.py:138
  218.6 1.2 add_convert_fusion
  224.7 5.5 %all-to-all-start.2 = ((bf16[8,2,1,32,512]{4,3,1,2,0:T(8,128)(2,1)}), bf16[8,2,1,32,512]{4,3,1,2,0:T(8,128)(2,1)S(1)}, u32[]{:S(2)}, u32[]{:S(2)}) async-start(bf16[8,2,1,32,512]{4,3,1,2,0:T(8,128)(2,1)} %fusion.27), calls=%async_computation.4 | async-start | bytes 1048576 | tf_op jit(solution)/shard_map/all_to_all | solution.py:143
  230.6 14.0 %all-to-all-done.2 = bf16[8,2,1,32,512]{4,3,1,2,0:T(8,128)(2,1)S(1)} async-done(((bf16[8,2,1,32,512]{4,3,1,2,0:T(8,128)(2,1)}), bf16[8,2,1,32,512]{4,3,1,2,0:T(8,128)(2,1)S(1)}, u32[]{:S(2)}, u32[]{:S(2)}) %all-to-all-start.2) | async-done | bytes 524320 | tf_op jit(solution)/shard_map/all_to_all | solution.py:143
  245.3 18.0 %all_to_all.44 = bf16[8,2,32,512]{3,2,1,0:T(8,128)(2,1)S(1)} all-to-all(bf16[8,2,32,512]{3,2,1,0:T(8,128)(2,1)S(1)} %bitcast.168), channel_id=1, replica_groups=mesh['seq'=8,'head'=4] {'seq'}, dimensions={0} | all-to-all | bytes 1048576 | tf_op jit(solution)/shard_map/all_to_all | solution.py:153
  263.4 0.8 slice_bitcast_fusion
  (85 shorter events, 10.1 us)
Async XLA Ops:
  7.2 171.3 %copy-start = (bf16[512,2048]{1,0:T(8,128)(2,1)S(1)}, bf16[512,2048]{1,0:T(8,128)(2,1)}, u32[]{:S(2)}) copy-start(bf16[512,2048]{1,0:T(8,128)(2,1)} %param.27) | copy-start | bytes 6291460
  7.2 38.8 %copy-start.4 = (bf16[256,512]{1,0:T(8,128)(2,1)S(1)}, bf16[256,512]{1,0:T(8,128)(2,1)}, u32[]{:S(2)}) copy-start(bf16[256,512]{1,0:T(8,128)(2,1)} %param.18) | copy-start | bytes 786436
  7.2 45.3 %copy-start.9 = (s32[8]{0:T(128)S(1)}, s32[8]{0:T(128)}, u32[]{:S(2)}) copy-start(s32[8]{0:T(128)} %param.19) | copy-start | bytes 100
  7.2 37.7 %reduce-scatter.3.cloned.1.call-start = ((), (), s32[]{:S(2)}) async-start(), calls=%async_computation.6 | async-start | bytes 2621440 | tf_op jit(solution)/shard_map/reduce_scatter | solution.py:71
  46.8 41.0 %copy-start.1 = (f32[8]{0:T(128)S(1)}, f32[8]{0:T(128)}, u32[]{:S(2)}) copy-start(f32[8]{0:T(128)} %param.20) | copy-start | bytes 100
  46.8 41.8 %copy-start.8 = (f32[4]{0:T(128)S(1)}, f32[4]{0:T(128)}, u32[]{:S(2)}) copy-start(f32[4]{0:T(128)} %param.25) | copy-start | bytes 52
  46.8 20.0 %all-to-all-start = ((bf16[2,8,32,512]{3,2,0,1:T(8,128)(2,1)}), bf16[2,8,32,512]{3,2,0,1:T(8,128)(2,1)S(1)}, u32[]{:S(2)}, u32[]{:S(2)}) async-start(bf16[2,8,32,512]{3,2,0,1:T(8,128)(2,1)} %pad_maximum_fusion), calls=%async_computation.1 | async-start | bytes 1048576 | tf_op jit(solution)/shard_map/all_to_all | solution.py:75
  52.5 54.8 %all-gather.5.cloned.1.call-start = ((), (), s32[]{:S(2)}) async-start(), calls=%async_computation.7 | async-start | bytes 2621440 | tf_op jit(solution)/shard_map/all_gather | solution.py:83
  86.5 89.5 %all-gather.7.cloned.1.call-start = ((), (), s32[]{:S(2)}) async-start(), calls=%async_computation.9 | async-start | bytes 1179648 | tf_op jit(solution)/shard_map/all_gather | solution.py:13
  88.6 20.8 %copy-start.6 = (bf16[2048,4]{0,1:T(4,128)(2,1)S(1)}, bf16[2048,4]{0,1:T(4,128)(2,1)}, u32[]{:S(2)}) copy-start(bf16[2048,4]{0,1:T(4,128)(2,1)} %param.24) | copy-start | bytes 49156
  88.6 20.8 %copy-start.7 = (f32[2048]{0:T(1024)S(1)}, f32[2048]{0:T(1024)}, u32[]{:S(2)}) copy-start(f32[2048]{0:T(1024)} %param.22) | copy-start | bytes 24580
  135.5 83.0 %reduce-scatter.5.cloned.1.call-start = ((), (), s32[]{:S(2)}) async-start(), calls=%async_computation.8 | async-start | bytes 2621440 | tf_op jit(solution)/shard_map/reduce_scatter | solution.py:138
  157.7 18.3 %copy-start.3 = (bf16[512,1,4,128]{3,2,1,0:T(4,128)(2,1)S(1)}, bf16[512,1,4,128]{3,2,1,0:T(4,128)(2,1)}, u32[]{:S(2)}) copy-start(bf16[512,1,4,128]{3,2,1,0:T(4,128)(2,1)} %get-tuple-element.106) | copy-start | bytes 1572868
  162.2 15.9 %copy-start.5 = (f32[4,128]{1,0:T(4,128)S(1)}, f32[4,128]{1,0:T(4,128)}, u32[]{:S(2)}) copy-start(f32[4,128]{1,0:T(4,128)} %param.26) | copy-start | bytes 6148
  178.4 40.1 %copy-start.2 = (bf16[1,2,8,32,512]{4,3,2,1,0:T(8,128)(2,1)S(1)}, bf16[1,2,8,32,512]{4,3,2,1,0:T(8,128)(2,1)}, u32[]{:S(2)}) copy-start(bf16[1,2,8,32,512]{4,3,2,1,0:T(8,128)(2,1)} %copy.187) | copy-start | bytes 1572868
  224.7 19.8 %all-to-all-start.2 = ((bf16[8,2,1,32,512]{4,3,1,2,0:T(8,128)(2,1)}), bf16[8,2,1,32,512]{4,3,1,2,0:T(8,128)(2,1)S(1)}, u32[]{:S(2)}, u32[]{:S(2)}) async-start(bf16[8,2,1,32,512]{4,3,1,2,0:T(8,128)(2,1)} %fusion.27), calls=%async_computation.4 | async-start | bytes 1048576 | tf_op jit(solution)/shard_map/all_to_all | solution.py:143
Sparse Core Ops, SparseCore 0:
  11.0 33.8 reduce-scatter.2
  86.6 20.6 all-gather.4
  135.6 40.3 all-gather.6
  181.2 37.2 reduce-scatter.4
